TPU v7x, 32 devices: a whole 2x2x4 slice. The times are simulated.
32 devices in a mesh: blk: 8 (over z, x), rep: 4 (over y, core).
Axes of the slice: x: 2, y: 2, z: 4, core: 2. Of those that a mesh axis runs over, the one named last changes fastest.
Arguments:
- embeddings: float32 [16384, 768], P(('blk', 'rep')), may hold values from -6 to 6
- ranks: int32 [16384], replicated, may hold values from 0 to 16383, each once
Outputs:
- earlier_best: float32 [16384], P(('blk', 'rep'))
- later_best: float32 [16384], P(('blk', 'rep'))
Inputs may be any that keep to these rules, and one draw needn't show every extreme that they name: ranks is a permutation of 0 .. 16383.
All inputs are finite; a program needn't handle non-finite values.
Results may differ from a plain program's by a relative error of at most 0.0012.
Values may be sent and summed in bfloat16 or wider, within the bound.
A program may use at most 64 MiB of HBM per device.

v0:
```python
import jax
import jax.numpy as jnp
from jax import lax
from jax.sharding import PartitionSpec as P

STEPS = 3


def shifted(value, axis, steps):
    count = lax.axis_size(axis)
    pairs = [(source, (source + steps) % count) for source in range(count)]
    return lax.ppermute(value, axis, pairs)


def best_pair(host, host_rank, visit, visit_rank):
    scores = lax.dot_general(
        host, visit, (((1,), (1,)), ((), ())), preferred_element_type=jnp.float32
    )
    kept = jnp.where(visit_rank[None, :] < host_rank[:, None], scores, jnp.float32(-1.0))
    return (jnp.max(kept, axis=1), jnp.max(kept, axis=0))


def shards(embeddings, ranks):
    rows = embeddings.shape[0]
    copies = lax.axis_size("rep")
    blocks = lax.axis_size("blk")
    span = rows * copies
    block_id = lax.axis_index("blk")
    copy_id = lax.axis_index("rep")
    squares = jnp.sum(embeddings * embeddings, axis=1, keepdims=True)
    unit = (embeddings * lax.rsqrt(squares + 1e-06)).astype(jnp.bfloat16)
    mine = copy_id * rows
    host = lax.all_gather(unit, "rep", axis=0, tiled=True)
    host_ranks = lax.dynamic_slice_in_dim(ranks, block_id * span, span)
    row_best = jnp.full((host.shape[0],), -1.0, jnp.float32)
    running = jnp.full((rows,), -1.0, jnp.float32)
    visit = unit
    part = unit
    for offset in range(STEPS + 1):
        if offset > 0:
            part = shifted(part, "blk", 1)
        visit = part
        start = (block_id - offset) % blocks * span + mine
        visit_rank = lax.dynamic_slice_in_dim(ranks, start, rows)
        row_part, column_part = best_pair(host, host_ranks, visit, visit_rank)
        row_best = jnp.maximum(row_best, row_part)
        if offset > 0:
            running = shifted(running, "blk", 1)
        running = jnp.maximum(running, column_part)
    home = shifted(running, "blk", -STEPS)
    row_merged = lax.pmax(row_best, "rep")
    return (lax.dynamic_slice_in_dim(row_merged, mine, rows), home)


def solution(mesh):
    return jax.shard_map(
        shards,
        mesh=mesh,
        in_specs=(P(("blk", "rep"), None), P()),
        out_specs=(P(("blk", "rep")), P(("blk", "rep"))),
        check_vma=False,
    )
```

profile of v0, /device:TPU:0, one launch (start us, length us, event | category | flops | bytes accessed | tf_op | source)
XLA Modules:
  0.0 113.6 jit_solution(10302306935951513888)
XLA Ops:
  7.2 0.0 copy-start.1
  7.2 0.0 all-gather.2.cloned.1.call-start
  7.2 1.6 %multiply_reduce_fusion = f32[512]{0:T(512)S(1)} fusion(f32[512,768]{1,0:T(8,128)} %param.2), kind=kLoop, calls=%fused_computation.13 | loop fusion | flops 785920 | bytes 1574912 | tf_op jit(solution)/shard_map/reduce_sum | solution.py:30
  8.8 2.4 %multiply_convert_fusion = bf16[512,768]{1,0:T(8,128)(2,1)} fusion(f32[512,768]{1,0:T(8,128)} %param.2, f32[512]{0:T(512)S(1)} %add_rsqrt_fusion), kind=kLoop, calls=%fused_computation.12 | loop fusion | flops 786432 | bytes 2361344 | tf_op jit(solution)/shard_map/convert_element_type | solution.py:31
  11.3 0.0 all-gather.2.cloned.1.call-update
  11.3 3.0 %collective-permute-start = (bf16[512,768]{1,0:T(8,128)(2,1)}, bf16[512,768]{1,0:T(8,128)(2,1)S(1)}, u32[]{:S(2)}, u32[]{:S(2)}) collective-permute-start(bf16[512,768]{1,0:T(8,128)(2,1)} %multiply_convert_fusion), channel_id=1, source_target_pairs={{0,4},{4,8},{8,12},{12,16},{16,20},{20,24},{24,28},{28,0},{1,5},{5... | collective-permute-start | bytes 2359304 | tf_op jit(solution)/shard_map/ppermute | solution.py:12
  14.3 20.8 %collective-permute-done = bf16[512,768]{1,0:T(8,128)(2,1)S(1)} collective-permute-done((bf16[512,768]{1,0:T(8,128)(2,1)}, bf16[512,768]{1,0:T(8,128)(2,1)S(1)}, u32[]{:S(2)}, u32[]{:S(2)}) %collective-permute-start) | collective-permute-done | bytes 786464 | tf_op jit(solution)/shard_map/ppermute | solution.py:12
  35.1 0.0 collective-permute-start.1
  35.1 0.0 copy-done.1
  35.1 0.1 fusion.8
  35.2 21.3 %collective-permute-done.1 = bf16[512,768]{1,0:T(8,128)(2,1)S(1)} collective-permute-done((bf16[512,768]{1,0:T(8,128)(2,1)S(1)}, bf16[512,768]{1,0:T(8,128)(2,1)S(1)}, u32[]{:S(2)}, u32[]{:S(2)}) %collective-permute-start.1) | collective-permute-done | bytes 786464 | tf_op jit(solution)/shard_map/ppermute | solution.py:12
  56.5 0.0 collective-permute-start.2
  56.5 3.9 %fusion.11 = f32[2048,512]{1,0:T(8,128)S(1)} fusion(bf16[2048,768]{1,0:T(8,128)(2,1)} %all-gather.2.cloned.1.call-done, bf16[512,768]{1,0:T(8,128)(2,1)S(1)} %collective-permute-done.1), kind=kOutput, calls=%fused_computation.20 | convolution fusion | flops 1610612736 | bytes 8126464 | tf_op jit(solution)/shard_map/dot_general | solution.py:16
  60.4 0.0 copy-done.2
  60.4 0.0 copy-start
  60.4 1.8 %fusion.10 = f32[2048,512]{1,0:T(8,128)S(1)} fusion(bf16[2048,768]{1,0:T(8,128)(2,1)S(1)} %copy-done.2, bf16[512,768]{1,0:T(8,128)(2,1)S(1)} %collective-permute-done), kind=kOutput, calls=%fused_computation.19 | convolution fusion | flops 1610612736 | bytes 8126464 | tf_op jit(solution)/shard_map/dot_general | solution.py:16
  62.2 0.0 dynamic-slice-start
  62.3 1.8 %fusion.9 = f32[2048,512]{1,0:T(8,128)S(1)} fusion(bf16[2048,768]{1,0:T(8,128)(2,1)S(1)} %copy-done.2, bf16[512,768]{1,0:T(8,128)(2,1)S(1)} %copy-done), kind=kOutput, calls=%fused_computation.18 | convolution fusion | flops 1610612736 | bytes 8126464 | tf_op jit(solution)/shard_map/dot_general | solution.py:16
  64.1 12.9 %collective-permute-done.2 = bf16[512,768]{1,0:T(8,128)(2,1)S(1)} collective-permute-done((bf16[512,768]{1,0:T(8,128)(2,1)S(1)}, bf16[512,768]{1,0:T(8,128)(2,1)S(1)}, u32[]{:S(2)}, u32[]{:S(2)}) %collective-permute-start.2) | collective-permute-done | bytes 786464 | tf_op jit(solution)/shard_map/ppermute | solution.py:12
  77.0 0.0 dynamic-slice-done
  77.0 3.7 %fusion.6 = (f32[512]{0:T(512)S(1)}, f32[2048]{0:T(1024)S(1)}, f32[2048]{0:T(1024)S(1)}, f32[512]{0:T(512)S(1)}, f32[2048]{0:T(1024)S(1)}, /*index=5*/f32[512]{0:T(512)S(1)}, f32[2048]{0:T(1024)S(1)}, f32[512]{0:T(512)S(1)}) fusion(s32[512]{0:T(512)S(1)} %get-tuple-element.19, s32[2048]{0:T(1024)S(1)} %dynamic-slice-done, f32[2048,512]{1,0:T(8,128)S(1)} %fusion.9, ...), kind=kOutput, calls=%fused_computation.10 | convolution fusion | flops 1627379712 | bytes 16572416 | tf_op jit(solution)/shard_map/dot_general | solution.py:16
  80.8 0.1 collective-permute-start.3
  80.9 6.3 %collective-permute-done.3 = f32[512]{0:T(512)S(1)} collective-permute-done((f32[512]{0:T(512)S(1)}, f32[512]{0:T(512)S(1)}, u32[]{:S(2)}, u32[]{:S(2)}) %collective-permute-start.3) | collective-permute-done | bytes 2080 | tf_op jit(solution)/shard_map/ppermute | solution.py:12
  87.1 0.0 collective-permute-start.4
  87.1 6.3 %collective-permute-done.4 = f32[512]{0:T(512)S(1)} collective-permute-done((f32[512]{0:T(512)S(1)}, f32[512]{0:T(512)S(1)}, u32[]{:S(2)}, u32[]{:S(2)}) %collective-permute-start.4) | collective-permute-done | bytes 2080 | tf_op jit(solution)/shard_map/ppermute | solution.py:12
  93.4 0.0 collective-permute-start.5
  93.4 6.3 %collective-permute-done.5 = f32[512]{0:T(512)S(1)} collective-permute-done((f32[512]{0:T(512)S(1)}, f32[512]{0:T(512)S(1)}, u32[]{:S(2)}, u32[]{:S(2)}) %collective-permute-start.5) | collective-permute-done | bytes 2080 | tf_op jit(solution)/shard_map/ppermute | solution.py:12
  99.7 0.0 collective-permute-start.6
  99.7 5.8 %pmax.7 = f32[2048]{0:T(1024)S(1)} all-reduce(f32[2048]{0:T(1024)S(1)} %maximum_maximum_fusion), channel_id=1, replica_groups=mesh['blk'=8,'rep'=4] {'rep'}, use_global_device_ids=true, to_apply=%region_5.6 | all-reduce | flops 2048 | bytes 16384 | tf_op jit(solution)/shard_map/pmax | solution.py:51
  105.5 0.7 dynamic_slice.23
  106.1 0.0 collective-permute-done.6
  106.1 0.6 copy.5
  (9 shorter events, 0.0 us)
Async XLA Ops:
  7.2 27.9 %copy-start.1 = (s32[16384]{0:T(1024)S(1)}, s32[16384]{0:T(1024)}, u32[]{:S(2)}) copy-start(s32[16384]{0:T(1024)} %param.3) | copy-start | bytes 196612
  7.2 49.3 %all-gather.2.cloned.1.call-start = ((), (), s32[]{:S(2)}) async-start(), calls=%async_computation | async-start | bytes 3932160 | tf_op jit(solution)/shard_map/all_gather | solution.py:33
  11.3 23.8 %collective-permute-start = (bf16[512,768]{1,0:T(8,128)(2,1)}, bf16[512,768]{1,0:T(8,128)(2,1)S(1)}, u32[]{:S(2)}, u32[]{:S(2)}) collective-permute-start(bf16[512,768]{1,0:T(8,128)(2,1)} %multiply_convert_fusion), channel_id=1, source_target_pairs={{0,4},{4,8},{8,12},{12,16},{16,20},{20,24},{24,28},{28,0},{1,5},{5... | collective-permute-start | bytes 2359304 | tf_op jit(solution)/shard_map/ppermute | solution.py:12
  35.1 21.4 %collective-permute-start.1 = (bf16[512,768]{1,0:T(8,128)(2,1)S(1)}, bf16[512,768]{1,0:T(8,128)(2,1)S(1)}, u32[]{:S(2)}, u32[]{:S(2)}) collective-permute-start(bf16[512,768]{1,0:T(8,128)(2,1)S(1)} %collective-permute-done), channel_id=1, source_target_pairs={{0,4},{4,8},{8,12},{12,16},{16,20},{20,24},{24,28},{28,0},{1,5},{5... | collective-permute-start | bytes 2359304 | tf_op jit(solution)/shard_map/ppermute | solution.py:12
  56.5 20.5 %collective-permute-start.2 = (bf16[512,768]{1,0:T(8,128)(2,1)S(1)}, bf16[512,768]{1,0:T(8,128)(2,1)S(1)}, u32[]{:S(2)}, u32[]{:S(2)}) collective-permute-start(bf16[512,768]{1,0:T(8,128)(2,1)S(1)} %collective-permute-done.1), channel_id=1, source_target_pairs={{0,4},{4,8},{8,12},{12,16},{16,20},{20,24},{24,28},{28,0},{1,5},{5... | collective-permute-start | bytes 2359304 | tf_op jit(solution)/shard_map/ppermute | solution.py:12
  56.5 3.9 %copy-start.2 = (bf16[2048,768]{1,0:T(8,128)(2,1)S(1)}, bf16[2048,768]{1,0:T(8,128)(2,1)}, u32[]{:S(2)}) copy-start(bf16[2048,768]{1,0:T(8,128)(2,1)} %all-gather.2.cloned.1.call-done) | copy-start | bytes 9437188
  60.4 1.9 %copy-start = (bf16[512,768]{1,0:T(8,128)(2,1)S(1)}, bf16[512,768]{1,0:T(8,128)(2,1)}, u32[]{:S(2)}) copy-start(bf16[512,768]{1,0:T(8,128)(2,1)} %multiply_convert_fusion) | copy-start | bytes 2359300
  62.2 14.8 %dynamic-slice-start = ((s32[16384]{0:T(1024)}, s32[]{:T(128)}), s32[2048]{0:T(1024)S(1)}, s32[]{:S(2)}) async-start(s32[16384]{0:T(1024)} %param.3, s32[]{:T(128)} %select_n.52), calls=%async_computation.1 | async-start | bytes 16896 | tf_op jit(solution)/shard_map/dynamic_slice | solution.py:34
  80.8 6.3 %collective-permute-start.3 = (f32[512]{0:T(512)S(1)}, f32[512]{0:T(512)S(1)}, u32[]{:S(2)}, u32[]{:S(2)}) collective-permute-start(f32[512]{0:T(512)S(1)} %broadcast_maximum_fusion), channel_id=1, source_target_pairs={{0,4},{4,8},{8,12},{12,16},{16,20},{20,24},{24,28},{28,0},{1,5},{5... | collective-permute-start | bytes 6152 | tf_op jit(solution)/shard_map/ppermute | solution.py:12
  87.1 6.3 %collective-permute-start.4 = (f32[512]{0:T(512)S(1)}, f32[512]{0:T(512)S(1)}, u32[]{:S(2)}, u32[]{:S(2)}) collective-permute-start(f32[512]{0:T(512)S(1)} %max.23), channel_id=1, source_target_pairs={{0,4},{4,8},{8,12},{12,16},{16,20},{20,24},{24,28},{28,0},{1,5},{5... | collective-permute-start | bytes 6152 | tf_op jit(solution)/shard_map/ppermute | solution.py:12
  93.4 6.3 %collective-permute-start.5 = (f32[512]{0:T(512)S(1)}, f32[512]{0:T(512)S(1)}, u32[]{:S(2)}, u32[]{:S(2)}) collective-permute-start(f32[512]{0:T(512)S(1)} %max.24), channel_id=1, source_target_pairs={{0,4},{4,8},{8,12},{12,16},{16,20},{20,24},{24,28},{28,0},{1,5},{5... | collective-permute-start | bytes 6152 | tf_op jit(solution)/shard_map/ppermute | solution.py:12
  99.7 6.4 %collective-permute-start.6 = (f32[512]{0:T(512)S(1)}, f32[512]{0:T(512)S(1)}, u32[]{:S(2)}, u32[]{:S(2)}) collective-permute-start(f32[512]{0:T(512)S(1)} %max.25), channel_id=1, source_target_pairs={{0,20},{4,24},{8,28},{12,0},{16,4},{20,8},{24,12},{28,16},{1,21},{... | collective-permute-start | bytes 6152 | tf_op jit(solution)/shard_map/ppermute | solution.py:12
Sparse Core Ops, SparseCore 0:
  11.4 31.2 all-gather.1
where the time goes:
time: 114 us
  waiting for transfers between devices  73.9 us (65%)
  between operations  14.1 us (12%)
  matrix products  11.3 us (10%)
  blocking collectives  5.75 us (5%)
  other arithmetic  4.05 us (4%)
  starting transfers between devices  3.13 us (3%)
  local copies, waits for them, and re-layouts  1.34 us (1%)
    ppermute x7, waiting for transfers between devices, shifted(): return lax.ppermute(value, axis, pairs)  73.9 us
    dot_general x4, matrix products, best_pair(): lax.dot_general(host, visit, (((1,), (1,)), ((), ())), preferred_element_...  11.3 us
    pmax x1, blocking collectives, shards(): row_merged = lax.pmax(row_best, 'rep')  5.75 us
    ppermute x7, starting transfers between devices, shifted(): return lax.ppermute(value, axis, pairs)  3.09 us
    convert_element_type x1, other arithmetic, shards(): unit = (embeddings * lax.rsqrt(squares + 1e-06)).astype(jnp.bfloat16)  2.44 us
  transfers between devices with their start and end apart: 8, of which 6 were waited for; matrix products, arithmetic and copies ran while one was open for 7% of the time, Pallas kernels for 0%

commit v1 on v0

v1 whole, which is shorter than its diff:
```python
import functools

import jax
import jax.numpy as jnp
from jax import lax
from jax.experimental import pallas as pl
from jax.experimental.pallas import tpu as pltpu
from jax.sharding import PartitionSpec as P

STEPS = 3
CHUNKS = 4
MESH = pl.DeviceIdType.MESH


def kernel(
    blocks, copies, emb_ref, ranks_ref, early_ref, late_ref,
    host, visit, host_rank, visit_rank, row_acc, col_acc, col_in, row_out, row_in,
    z_send, x_send, y_send, core_send, two_send, one_send, relay_send, col_send, row_send,
    visit_recv, y_recv, core_recv, relay_recv, col_recv, row_recv,
):
    rows = emb_ref.shape[0]
    part = rows // CHUNKS
    b = lax.axis_index("blk")
    r = lax.axis_index("rep")
    odd = lax.rem(b, 2)
    even = odd == 0

    def blk(offset):
        return lax.rem(b + offset + blocks, blocks)

    core = r + 1 - 2 * lax.rem(r, 2)
    far = lax.rem(r + copies // 2, copies)
    far_core = lax.rem(core + copies // 2, copies)
    peers = (core, far, far_core)

    barrier = pltpu.get_barrier_semaphore()
    for offset in (1, 2, 3, -1, -2, -3):
        pl.semaphore_signal(barrier, inc=1, device_id=(blk(offset), r), device_id_type=MESH)
    for peer in peers:
        pl.semaphore_signal(barrier, inc=1, device_id=(b, peer), device_id_type=MESH)

    def normalise(i, _):
        at = pl.ds(pl.multiple_of(i * 64, 64), 64)
        x = emb_ref[at, :]
        squares = jnp.sum(x * x, axis=1, keepdims=True)
        host[0, at, :] = (x * lax.rsqrt(squares + 1e-06)).astype(jnp.bfloat16)
        return 0

    lax.fori_loop(0, rows // 64, normalise, 0)

    def cut(i):
        return pl.ds(pl.multiple_of(i * part, part), part)

    pl.semaphore_wait(barrier, 9)

    def send(src, dst, send_sem, recv_sem, device):
        copy = pltpu.make_async_remote_copy(
            src_ref=src, dst_ref=dst, send_sem=send_sem, recv_sem=recv_sem,
            device_id=device, device_id_type=MESH,
        )
        return copy

    def z_copy(i):
        return send(host.at[0, cut(i)], visit.at[1, cut(i)], z_send.at[i],
                    visit_recv.at[1, i], (blk(2), r))

    def x_copy(i):
        return send(host.at[0, cut(i)], visit.at[0, cut(i)], x_send.at[i],
                    visit_recv.at[0, i], (blk(1), r))

    def y_copy(i):
        return send(host.at[0, cut(i)], host.at[2, cut(i)], y_send.at[i],
                    y_recv.at[i], (b, far))

    def core_copy():
        return send(host.at[0], host.at[1], core_send, core_recv, (b, core))

    def relay_copy(i):
        return send(host.at[2, cut(i)], host.at[3, cut(i)], relay_send.at[i],
                    relay_recv.at[i], (b, core))

    def two_copy(i):
        slot = 2 - 2 * odd
        return send(visit.at[1, cut(i)], visit.at[slot, cut(i)], two_send.at[i],
                    visit_recv.at[slot, i], (blk(1 - 2 * odd), r))

    def one_copy(i):
        return send(visit.at[0, cut(i)], visit.at[2, cut(i)], one_send.at[i],
                    visit_recv.at[2, i], (blk(2), r))

    core_copy().start()
    for i in range(CHUNKS):
        z_copy(i).start()
        y_copy(i).start()

        @pl.when(even)
        def _():
            x_copy(i).start()

    owners = (r,) + peers
    for h, owner in enumerate(owners):
        line = ranks_ref[pl.ds(b * copies + owner, 1), :]
        host_rank[h] = jnp.broadcast_to(line, (128, rows)).T
    for slot, offset in enumerate((1, 2, 3, 0)):
        line = ranks_ref[pl.ds(blk(-offset) * copies + r, 1), :]
        visit_rank[slot] = jnp.broadcast_to(line, (8, rows))
    row_acc[...] = jnp.full(row_acc.shape, -1.0, jnp.float32)
    col_acc[...] = jnp.full(col_acc.shape, -1.0, jnp.float32)

    def score(other, slot, start, size, h):
        at = pl.ds(pl.multiple_of(start, size), size)
        scores = lax.dot_general(
            host[h], other[at, :], (((1,), (1,)), ((), ())),
            preferred_element_type=jnp.float32,
        )
        line = visit_rank[slot, 0:1, at]
        best = row_acc[h]
        for g in range(size // 128):
            kept = jnp.where(
                line[:, g * 128:(g + 1) * 128] < host_rank[h],
                scores[:, g * 128:(g + 1) * 128], jnp.float32(-1.0),
            )
            best = jnp.maximum(best, kept)
            column = jnp.max(kept.reshape(rows // 8, 8, 128), axis=0)
            there = pl.ds(pl.multiple_of(start + g * 128, 128), 128)
            col_acc[slot, :, there] = jnp.maximum(col_acc[slot, :, there], column)
        row_acc[h] = best

    wide = 256

    def sweep(other, slot, low, high):
        def step(t, _):
            h = low + t // (rows // wide)
            c = lax.rem(t, rows // wide)
            score(other, slot, c * wide, wide, h)
            return 0
        lax.fori_loop(0, (high - low) * (rows // wide), step, 0)

    sweep(host.at[0], 3, 0, 1)
    core_copy().wait_recv()
    sweep(host.at[0], 3, 1, 2)

    def arrive(i, _):
        y_copy(i).wait_recv()
        relay_copy(i).start()
        z_copy(i).wait_recv()
        two_copy(i).start()
        lax.fori_loop(0, 2, lambda h, c: (score(visit.at[1], 1, i * part, part, h), c)[1], 0)
        x_copy(i).wait_recv()

        @pl.when(even)
        def _():
            one_copy(i).start()

        lax.fori_loop(0, 2, lambda h, c: (score(visit.at[0], 0, i * part, part, h), c)[1], 0)
        return 0

    lax.fori_loop(0, CHUNKS, arrive, 0)
    for i in range(CHUNKS):
        relay_copy(i).wait_recv()
    sweep(host.at[0], 3, 2, 4)
    sweep(visit.at[1], 1, 2, 4)
    sweep(visit.at[0], 0, 2, 4)

    def col_copy(k):
        return send(col_acc.at[k], col_in.at[k], col_send.at[k], col_recv.at[k],
                    (blk(-1 - k), r))

    def last(i, _):
        one_copy(i).wait_recv()
        lax.fori_loop(0, 4, lambda h, c: (score(visit.at[2], 2, i * part, part, h), c)[1], 0)
        return 0

    col_copy(1).start()
    col_copy(0).start()
    lax.fori_loop(0, CHUNKS, last, 0)
    col_copy(2).start()

    def row_copy(k):
        return send(row_out.at[k], row_in.at[k], row_send.at[k], row_recv.at[k], (b, peers[k]))

    for k in range(3):
        best = jnp.max(row_acc[k + 1].T.reshape(16, 8, rows), axis=0)
        row_out[k] = best
        row_copy(k).start()

    early = jnp.max(row_acc[0].T.reshape(16, 8, rows), axis=0)
    late = col_acc[3]
    for k in range(3):
        row_copy(k).wait_recv()
        early = jnp.maximum(early, row_in[k])
    for k in range(3):
        col_copy(k).wait_recv()
        late = jnp.maximum(late, col_in[k])
    early_ref[...] = jnp.max(early, axis=0, keepdims=True)
    late_ref[...] = jnp.max(late, axis=0, keepdims=True)

    core_copy().wait_send()

    def drain(i, _):
        z_copy(i).wait_send()
        y_copy(i).wait_send()
        relay_copy(i).wait_send()
        two_copy(i).wait_send()

        @pl.when(even)
        def _():
            x_copy(i).wait_send()
            one_copy(i).wait_send()
        return 0

    lax.fori_loop(0, CHUNKS, drain, 0)
    for k in range(3):
        col_copy(k).wait_send()
        row_copy(k).wait_send()


def shards(embeddings, ranks):
    rows, width = embeddings.shape
    copies = lax.axis_size("rep")
    blocks = lax.axis_size("blk")
    lines = ranks.reshape(-1, rows)
    dma = pltpu.SemaphoreType.DMA
    vmem = pl.BlockSpec(memory_space=pltpu.VMEM)
    early, late = pl.pallas_call(
        functools.partial(kernel, blocks, copies),
        out_shape=[jax.ShapeDtypeStruct((1, rows), jnp.float32)] * 2,
        in_specs=[vmem, vmem],
        out_specs=[vmem, vmem],
        scratch_shapes=[
            pltpu.VMEM((4, rows, width), jnp.bfloat16),
            pltpu.VMEM((STEPS, rows, width), jnp.bfloat16),
            pltpu.VMEM((4, rows, 128), jnp.int32),
            pltpu.VMEM((4, 8, rows), jnp.int32),
            pltpu.VMEM((4, rows, 128), jnp.float32),
            pltpu.VMEM((4, 8, rows), jnp.float32),
            pltpu.VMEM((3, 8, rows), jnp.float32),
            pltpu.VMEM((3, 8, rows), jnp.float32),
            pltpu.VMEM((3, 8, rows), jnp.float32),
            dma((CHUNKS,)), dma((CHUNKS,)), dma((CHUNKS,)), dma,
            dma((CHUNKS,)), dma((CHUNKS,)), dma((CHUNKS,)), dma((3,)), dma((3,)),
            dma((STEPS, CHUNKS)), dma((CHUNKS,)), dma, dma((CHUNKS,)), dma((3,)), dma((3,)),
        ],
        compiler_params=pltpu.CompilerParams(
            collective_id=0, has_side_effects=True, vmem_limit_bytes=32 * 1024 * 1024
        ),
    )(embeddings, lines)
    return early.reshape(rows), late.reshape(rows)


def solution(mesh):
    return jax.shard_map(
        shards,
        mesh=mesh,
        in_specs=(P(("blk", "rep"), None), P()),
        out_specs=(P(("blk", "rep")), P(("blk", "rep"))),
        check_vma=False,
    )
```

time: 114 us -> 50.9 us (0.45)
  waiting for transfers between devices: 73.9 us -> 0 us
  Pallas kernels: 0 us -> 46.7 us
  between operations: 14.1 us -> 0.65 us
  matrix products: 11.3 us -> 0 us
  blocking collectives: 5.75 us -> 0 us
  other arithmetic: 4.05 us -> 0 us
  starting transfers between devices: 3.13 us -> 0 us
  local copies, waits for them, and re-layouts: 1.34 us -> 3.41 us
    ppermute x7 -> x0, waiting for transfers between devices: 73.9 us -> none  [shifted(): return lax.ppermute(value, axis, pairs)]
    pallas_call x0 -> x1, Pallas kernels: none -> 46.7 us  [shards(): pl.pallas_call(functools.partial(kernel, blocks, copies), out_shape=[jax....]
    dot_general x4 -> x0, matrix products: 11.3 us -> none  [best_pair(): lax.dot_general(host, visit, (((1,), (1,)), ((), ())), preferred_element_...]
    pmax x1 -> x0, blocking collectives: 5.75 us -> none  [shards(): row_merged = lax.pmax(row_best, 'rep')]
    ppermute x7 -> x0, starting transfers between devices: 3.09 us -> none  [shifted(): return lax.ppermute(value, axis, pairs)]
    convert_element_type x1 -> x0, other arithmetic: 2.44 us -> none  [shards(): unit = (embeddings * lax.rsqrt(squares + 1e-06)).astype(jnp.bfloat16)]
    unnamed x7 -> x4, local copies, waits for them, and re-layouts: 0.59 us -> 2.56 us
    reduce_sum x1 -> x0, other arithmetic: 1.59 us -> none  [shards(): squares = jnp.sum(embeddings * embeddings, axis=1, keepdims=True)]
  transfers between devices with their start and end apart: 8 -> 0, of which waited for: 6 -> 0; matrix products, arithmetic and copies ran while one was open for 7% -> 0% of each run, Pallas kernels for 0% -> 0%
where the time goes in v1:
time: 50.9 us; the launch traced here: 50.7 us
  Pallas kernels  46.7 us (92%)
  local copies, waits for them, and re-layouts  3.41 us (7%)
  between operations  0.65 us (1%)
    pallas_call x1, Pallas kernels, shards(): pl.pallas_call(functools.partial(kernel, blocks, copies), out_shape=[jax....  46.7 us
    unnamed x4, local copies, waits for them, and re-layouts  2.56 us

profile of v1, /device:TPU:0, one launch (start us, length us, event | category | flops | bytes accessed | tf_op | source)
XLA Modules:
  0.0 50.7 jit_solution(17630896444168677964)
XLA Ops:
  0.6 0.9 %reshape.13.ranks_ref = s32[32,512]{1,0:T(8,128)S(1)} reshape(s32[16384]{0:T(1024)} %param.3) | data formatting | bytes 131072 | tf_op jit(solution)/shard_map/reshape | solution.py:222
  1.5 0.0 copy-start
  1.5 1.4 %copy-done = f32[512,768]{1,0:T(8,128)S(1)} copy-done((f32[512,768]{1,0:T(8,128)S(1)}, f32[512,768]{1,0:T(8,128)}, u32[]{:S(2)}) %copy-start) | copy-done | bytes 1572888
  2.9 46.7 %shard_map.41 = (f32[1,512]{1,0:T(1,128)S(1)}, f32[1,512]{1,0:T(1,128)S(1)}) custom-call(f32[512,768]{1,0:T(8,128)S(1)} %copy-done, s32[32,512]{1,0:T(8,128)S(1)} %reshape.13.ranks_ref), custom_call_target="tpu_custom_call" | custom-call | tf_op jit(solution)/shard_map/pallas_call | solution.py:225
  49.6 0.6 %copy.6 = f32[512]{0:T(512)} copy(f32[512]{0:T(512)S(1)} %bitcast.3) | data formatting | bytes 4096
  50.1 0.6 %copy.7 = f32[512]{0:T(512)} copy(f32[512]{0:T(512)S(1)} %bitcast.2) | data formatting | bytes 4096
Async XLA Ops:
  1.5 1.4 %copy-start = (f32[512,768]{1,0:T(8,128)S(1)}, f32[512,768]{1,0:T(8,128)}, u32[]{:S(2)}) copy-start(f32[512,768]{1,0:T(8,128)} %emb_ref.1) | copy-start | bytes 4718596

commit v2 on v1

--- a/solution.py
+++ b/solution.py
@@ -14,7 +14,7 @@
 
 def kernel(
     blocks, copies, emb_ref, ranks_ref, early_ref, late_ref,
-    host, visit, host_rank, visit_rank, row_acc, col_acc, col_in, row_out, row_in,
+    emb, load_sem, host, visit, host_rank, visit_rank, row_acc, col_acc, col_in, row_out, row_in,
     z_send, x_send, y_send, core_send, two_send, one_send, relay_send, col_send, row_send,
     visit_recv, y_recv, core_recv, relay_recv, col_recv, row_recv,
 ):
@@ -39,19 +39,11 @@
     for peer in peers:
         pl.semaphore_signal(barrier, inc=1, device_id=(b, peer), device_id_type=MESH)
 
-    def normalise(i, _):
-        at = pl.ds(pl.multiple_of(i * 64, 64), 64)
-        x = emb_ref[at, :]
-        squares = jnp.sum(x * x, axis=1, keepdims=True)
-        host[0, at, :] = (x * lax.rsqrt(squares + 1e-06)).astype(jnp.bfloat16)
-        return 0
-
-    lax.fori_loop(0, rows // 64, normalise, 0)
-
     def cut(i):
         return pl.ds(pl.multiple_of(i * part, part), part)
 
-    pl.semaphore_wait(barrier, 9)
+    for i in range(CHUNKS):
+        pltpu.make_async_copy(emb_ref.at[cut(i)], emb.at[cut(i)], load_sem.at[i]).start()
 
     def send(src, dst, send_sem, recv_sem, device):
         copy = pltpu.make_async_remote_copy(
@@ -88,8 +80,18 @@
         return send(visit.at[0, cut(i)], visit.at[2, cut(i)], one_send.at[i],
                     visit_recv.at[2, i], (blk(2), r))
 
-    core_copy().start()
-    for i in range(CHUNKS):
+    def load(i):
+        return pltpu.make_async_copy(emb_ref.at[cut(i)], emb.at[cut(i)], load_sem.at[i])
+
+    def normalise(i):
+        load(i).wait()
+        for j in range(part // 32):
+            at = pl.ds(i * part + j * 32, 32)
+            x = emb[at, :]
+            squares = jnp.sum(x * x, axis=1, keepdims=True)
+            host[0, at, :] = (x * lax.rsqrt(squares + 1e-06)).astype(jnp.bfloat16)
+
+    def spread(i):
         z_copy(i).start()
         y_copy(i).start()
 
@@ -97,15 +99,26 @@
         def _():
             x_copy(i).start()
 
-    owners = (r,) + peers
-    for h, owner in enumerate(owners):
-        line = ranks_ref[pl.ds(b * copies + owner, 1), :]
-        host_rank[h] = jnp.broadcast_to(line, (128, rows)).T
-    for slot, offset in enumerate((1, 2, 3, 0)):
-        line = ranks_ref[pl.ds(blk(-offset) * copies + r, 1), :]
-        visit_rank[slot] = jnp.broadcast_to(line, (8, rows))
+    lines = rows // 128
     row_acc[...] = jnp.full(row_acc.shape, -1.0, jnp.float32)
     col_acc[...] = jnp.full(col_acc.shape, -1.0, jnp.float32)
+    normalise(0)
+    normalise(1)
+    pl.semaphore_wait(barrier, 9)
+    spread(0)
+    for i in range(2, CHUNKS):
+        normalise(i)
+        spread(i - 1)
+    for slot, offset in enumerate((1, 2, 3, 0)):
+        for g in range(lines):
+            line = ranks_ref[pl.ds((blk(-offset) * copies + r) * lines + g, 1), :]
+            visit_rank[slot, :, g * 128:(g + 1) * 128] = jnp.broadcast_to(line, (8, 128))
+    spread(CHUNKS - 1)
+    core_copy().start()
+    for h, owner in enumerate((r,) + peers):
+        for g in range(lines):
+            line = ranks_ref[pl.ds((b * copies + owner) * lines + g, 1), :]
+            host_rank[h, g * 128:(g + 1) * 128, :] = jnp.broadcast_to(line, (128, 128)).T
 
     def score(other, slot, start, size, h):
         at = pl.ds(pl.multiple_of(start, size), size)
@@ -174,7 +187,6 @@
     col_copy(1).start()
     col_copy(0).start()
     lax.fori_loop(0, CHUNKS, last, 0)
-    col_copy(2).start()
 
     def row_copy(k):
         return send(row_out.at[k], row_in.at[k], row_send.at[k], row_recv.at[k], (b, peers[k]))
@@ -182,8 +194,10 @@
     for k in range(3):
         best = jnp.max(row_acc[k + 1].T.reshape(16, 8, rows), axis=0)
         row_out[k] = best
+
+    col_copy(2).start()
+    for k in range(3):
         row_copy(k).start()
-
     early = jnp.max(row_acc[0].T.reshape(16, 8, rows), axis=0)
     late = col_acc[3]
     for k in range(3):
@@ -219,15 +233,17 @@
     rows, width = embeddings.shape
     copies = lax.axis_size("rep")
     blocks = lax.axis_size("blk")
-    lines = ranks.reshape(-1, rows)
+    lines = ranks.reshape(-1, 128)
     dma = pltpu.SemaphoreType.DMA
     vmem = pl.BlockSpec(memory_space=pltpu.VMEM)
     early, late = pl.pallas_call(
         functools.partial(kernel, blocks, copies),
         out_shape=[jax.ShapeDtypeStruct((1, rows), jnp.float32)] * 2,
-        in_specs=[vmem, vmem],
+        in_specs=[pl.BlockSpec(memory_space=pltpu.HBM), vmem],
         out_specs=[vmem, vmem],
         scratch_shapes=[
+            pltpu.VMEM((rows, width), jnp.float32),
+            dma((CHUNKS,)),
             pltpu.VMEM((4, rows, width), jnp.bfloat16),
             pltpu.VMEM((STEPS, rows, width), jnp.bfloat16),
             pltpu.VMEM((4, rows, 128), jnp.int32),
@@ -242,7 +258,7 @@
             dma((STEPS, CHUNKS)), dma((CHUNKS,)), dma, dma((CHUNKS,)), dma((3,)), dma((3,)),
         ],
         compiler_params=pltpu.CompilerParams(
-            collective_id=0, has_side_effects=True, vmem_limit_bytes=32 * 1024 * 1024
+            collective_id=0, has_side_effects=True, vmem_limit_bytes=56 * 1024 * 1024
         ),
     )(embeddings, lines)
     return early.reshape(rows), late.reshape(rows)

time: 50.9 us -> 51.5 us (1.012)
  Pallas kernels: 46.7 us -> 48.2 us
  local copies, waits for them, and re-layouts: 3.41 us -> 2.48 us
    pallas_call x1, Pallas kernels: 46.7 us -> 48.2 us  [shards(): pl.pallas_call(functools.partial(kernel, blocks, copies), out_shape=[jax....]
    reshape x1 -> x0, local copies, waits for them, and re-layouts: 0.85 us -> none  [shards(): lines = ranks.reshape(-1, rows)]
    unnamed x4 -> x2, local copies, waits for them, and re-layouts: 2.56 us -> 2.48 us
where the time goes in v2:
time: 51.5 us; the launch traced here: 51.3 us
  Pallas kernels  48.2 us (94%)
  local copies, waits for them, and re-layouts  2.48 us (5%)
  between operations  0.64 us (1%)
    pallas_call x1, Pallas kernels, shards(): pl.pallas_call(functools.partial(kernel, blocks, copies), out_shape=[jax....  48.2 us
    unnamed x2, local copies, waits for them, and re-layouts  2.48 us

profile of v2, /device:TPU:0, one launch (start us, length us, event | category | flops | bytes accessed | tf_op | source)
XLA Modules:
  0.0 51.3 jit_solution(11864236500297212698)
XLA Ops:
  0.6 48.2 %shard_map.41 = (f32[1,512]{1,0:T(1,128)}, f32[1,512]{1,0:T(1,128)}) custom-call(f32[512,768]{1,0:T(8,128)} %emb_ref.1, s32[128,128]{1,0:T(8,128)} %bitcast.3), custom_call_target="tpu_custom_call" | custom-call | tf_op jit(solution)/shard_map/pallas_call | solution.py:239
  48.8 1.2 %copy.6 = f32[512]{0:T(512)} copy(f32[512]{0:T(512)} %bitcast.5) | data formatting | bytes 4096
  50.1 1.2 %copy.7 = f32[512]{0:T(512)} copy(f32[512]{0:T(512)} %bitcast.4) | data formatting | bytes 4096

commit v3 on v2

--- a/solution.py
+++ b/solution.py
@@ -34,8 +34,8 @@
     peers = (core, far, far_core)
 
     barrier = pltpu.get_barrier_semaphore()
-    for offset in (1, 2, 3, -1, -2, -3):
-        pl.semaphore_signal(barrier, inc=1, device_id=(blk(offset), r), device_id_type=MESH)
+    for other in (blk(2), blk(-2), b + 1 - 2 * odd):
+        pl.semaphore_signal(barrier, inc=1, device_id=(other, r), device_id_type=MESH)
     for peer in peers:
         pl.semaphore_signal(barrier, inc=1, device_id=(b, peer), device_id_type=MESH)
 
@@ -104,7 +104,7 @@
     col_acc[...] = jnp.full(col_acc.shape, -1.0, jnp.float32)
     normalise(0)
     normalise(1)
-    pl.semaphore_wait(barrier, 9)
+    pl.semaphore_wait(barrier, 6)
     spread(0)
     for i in range(2, CHUNKS):
         normalise(i)
@@ -120,34 +120,34 @@
             line = ranks_ref[pl.ds((b * copies + owner) * lines + g, 1), :]
             host_rank[h, g * 128:(g + 1) * 128, :] = jnp.broadcast_to(line, (128, 128)).T
 
-    def score(other, slot, start, size, h):
+    def score(other, slot, start, size, low, high):
         at = pl.ds(pl.multiple_of(start, size), size)
+        span = (high - low) * rows
         scores = lax.dot_general(
-            host[h], other[at, :], (((1,), (1,)), ((), ())),
+            host[low:high].reshape(span, host.shape[2]), other[at, :], (((1,), (1,)), ((), ())),
             preferred_element_type=jnp.float32,
         )
         line = visit_rank[slot, 0:1, at]
-        best = row_acc[h]
+        marks = host_rank[low:high].reshape(span, 128)
+        best = row_acc[low:high].reshape(span, 128)
         for g in range(size // 128):
             kept = jnp.where(
-                line[:, g * 128:(g + 1) * 128] < host_rank[h],
+                line[:, g * 128:(g + 1) * 128] < marks,
                 scores[:, g * 128:(g + 1) * 128], jnp.float32(-1.0),
             )
             best = jnp.maximum(best, kept)
-            column = jnp.max(kept.reshape(rows // 8, 8, 128), axis=0)
+            column = jnp.max(kept.reshape(span // 8, 8, 128), axis=0)
             there = pl.ds(pl.multiple_of(start + g * 128, 128), 128)
             col_acc[slot, :, there] = jnp.maximum(col_acc[slot, :, there], column)
-        row_acc[h] = best
+        row_acc[low:high] = best.reshape(high - low, rows, 128)
 
     wide = 256
 
     def sweep(other, slot, low, high):
-        def step(t, _):
-            h = low + t // (rows // wide)
-            c = lax.rem(t, rows // wide)
-            score(other, slot, c * wide, wide, h)
+        def step(c, _):
+            score(other, slot, c * wide, wide, low, high)
             return 0
-        lax.fori_loop(0, (high - low) * (rows // wide), step, 0)
+        lax.fori_loop(0, rows // wide, step, 0)
 
     sweep(host.at[0], 3, 0, 1)
     core_copy().wait_recv()
@@ -158,14 +158,14 @@
         relay_copy(i).start()
         z_copy(i).wait_recv()
         two_copy(i).start()
-        lax.fori_loop(0, 2, lambda h, c: (score(visit.at[1], 1, i * part, part, h), c)[1], 0)
+        score(visit.at[1], 1, i * part, part, 0, 2)
         x_copy(i).wait_recv()
 
         @pl.when(even)
         def _():
             one_copy(i).start()
 
-        lax.fori_loop(0, 2, lambda h, c: (score(visit.at[0], 0, i * part, part, h), c)[1], 0)
+        score(visit.at[0], 0, i * part, part, 0, 2)
         return 0
 
     lax.fori_loop(0, CHUNKS, arrive, 0)
@@ -181,7 +181,7 @@
 
     def last(i, _):
         one_copy(i).wait_recv()
-        lax.fori_loop(0, 4, lambda h, c: (score(visit.at[2], 2, i * part, part, h), c)[1], 0)
+        score(visit.at[2], 2, i * part, part, 0, 4)
         return 0
 
     col_copy(1).start()
@@ -258,7 +258,7 @@
             dma((STEPS, CHUNKS)), dma((CHUNKS,)), dma, dma((CHUNKS,)), dma((3,)), dma((3,)),
         ],
         compiler_params=pltpu.CompilerParams(
-            collective_id=0, has_side_effects=True, vmem_limit_bytes=56 * 1024 * 1024
+            collective_id=0, has_side_effects=True, vmem_limit_bytes=63 * 1024 * 1024
         ),
     )(embeddings, lines)
     return early.reshape(rows), late.reshape(rows)

time: 51.5 us -> 51 us (level)
  no operation moved by 1% of the time
where the time goes in v3:
time: 51 us; the launch traced here: 50.8 us
  Pallas kernels  47.7 us (94%)
  local copies, waits for them, and re-layouts  2.48 us (5%)
  between operations  0.64 us (1%)
    pallas_call x1, Pallas kernels, shards(): pl.pallas_call(functools.partial(kernel, blocks, copies), out_shape=[jax....  47.7 us
    unnamed x2, local copies, waits for them, and re-layouts  2.48 us

profile of v3, /device:TPU:0, one launch (start us, length us, event | category | flops | bytes accessed | tf_op | source)
XLA Modules:
  0.0 50.8 jit_solution(3823574031118817906)
XLA Ops:
  0.6 47.7 %shard_map.41 = (f32[1,512]{1,0:T(1,128)}, f32[1,512]{1,0:T(1,128)}) custom-call(f32[512,768]{1,0:T(8,128)} %emb_ref.1, s32[128,128]{1,0:T(8,128)} %bitcast.3), custom_call_target="tpu_custom_call" | custom-call | tf_op jit(solution)/shard_map/pallas_call | solution.py:239
  48.3 1.2 %copy.6 = f32[512]{0:T(512)} copy(f32[512]{0:T(512)} %bitcast.5) | data formatting | bytes 4096
  49.6 1.2 %copy.7 = f32[512]{0:T(512)} copy(f32[512]{0:T(512)} %bitcast.4) | data formatting | bytes 4096

commit v4 on v3

v4 whole, which is shorter than its diff:
```python
import functools

import jax
import jax.numpy as jnp
from jax import lax
from jax.experimental import pallas as pl
from jax.experimental.pallas import tpu as pltpu
from jax.sharding import PartitionSpec as P

CHUNKS = 4
MESH = pl.DeviceIdType.MESH


def kernel(
    blocks, copies, emb_ref, ranks_ref, early_ref, late_ref,
    emb, load_sem, host, visit, host_rank, visit_rank, row_acc, col_acc, col_in, row_out, row_in,
    z_send, x_send, y_send, core_send, relay_send, side_send, on_send, col_send, row_send,
    visit_recv, x_recv, y_recv, core_recv, relay_recv, col_recv, row_recv,
):
    rows = emb_ref.shape[0]
    part = rows // CHUNKS
    b = lax.axis_index("blk")
    r = lax.axis_index("rep")
    odd = lax.rem(b, 2)
    even = odd == 0

    def blk(offset):
        return lax.rem(b + offset + blocks, blocks)

    core = r + 1 - 2 * lax.rem(r, 2)
    far = lax.rem(r + copies // 2, copies)
    far_core = lax.rem(core + copies // 2, copies)
    peers = (core, far, far_core)

    barrier = pltpu.get_barrier_semaphore()
    for other in (blk(2), blk(-2), b + 1 - 2 * odd):
        pl.semaphore_signal(barrier, inc=1, device_id=(other, r), device_id_type=MESH)
    for peer in peers:
        pl.semaphore_signal(barrier, inc=1, device_id=(b, peer), device_id_type=MESH)

    def cut(i):
        return pl.ds(pl.multiple_of(i * part, part), part)

    for i in range(CHUNKS):
        pltpu.make_async_copy(emb_ref.at[cut(i)], emb.at[cut(i)], load_sem.at[i]).start()

    def send(src, dst, send_sem, recv_sem, device):
        copy = pltpu.make_async_remote_copy(
            src_ref=src, dst_ref=dst, send_sem=send_sem, recv_sem=recv_sem,
            device_id=device, device_id_type=MESH,
        )
        return copy

    def hrow(h, i):
        return pl.ds(pl.multiple_of(h * rows + i * part, part), part)

    keep = CHUNKS - 1
    across = b + 1 - 2 * odd

    def z_copy(i):
        return send(host.at[hrow(0, i)], visit.at[0, cut(i)], z_send.at[i],
                    visit_recv.at[0, i], (blk(2), r))

    def x_copy(i):
        return send(host.at[hrow(0, i)], host.at[hrow(4, i)], x_send.at[i],
                    x_recv.at[i], (across, r))

    def y_copy(i):
        return send(host.at[hrow(0, i)], host.at[hrow(2, i)], y_send.at[i],
                    y_recv.at[i], (b, far))

    def core_copy():
        return send(host.at[pl.ds(0, rows)], host.at[pl.ds(rows, rows)], core_send, core_recv,
                    (b, core))

    def relay_y(i):
        return send(host.at[hrow(2, i)], host.at[hrow(3, i)], relay_send.at[0, i],
                    relay_recv.at[0, i], (b, core))

    def relay_x(i):
        return send(host.at[hrow(4, i)], host.at[hrow(5, i)], relay_send.at[1, i],
                    relay_recv.at[1, i], (b, core))

    def side_copy(i):
        return send(visit.at[0, cut(i)], visit.at[1, cut(i)], side_send.at[i],
                    visit_recv.at[1, i], (across, r))

    def up_copy():
        return send(visit.at[0, cut(keep)], visit.at[2, cut(keep)], side_send.at[keep],
                    visit_recv.at[2, keep], (b, far))

    def on_copy(i):
        return send(visit.at[1, cut(i)], visit.at[3, cut(i)], on_send.at[i],
                    visit_recv.at[3, i], (blk(2), r))

    def on_v():
        return send(visit.at[0, cut(keep)], visit.at[3, cut(keep)], on_send.at[keep],
                    visit_recv.at[3, keep], (blk(2), r))

    def on_y():
        return send(visit.at[2, cut(keep)], visit.at[4, cut(keep)], on_send.at[keep + 1],
                    visit_recv.at[4, keep], (blk(2), r))

    def load(i):
        return pltpu.make_async_copy(emb_ref.at[cut(i)], emb.at[cut(i)], load_sem.at[i])

    def normalise(i):
        load(i).wait()
        for j in range(part // 32):
            at = pl.ds(i * part + j * 32, 32)
            x = emb[at, :]
            squares = jnp.sum(x * x, axis=1, keepdims=True)
            host[at, :] = (x * lax.rsqrt(squares + 1e-06)).astype(jnp.bfloat16)

    def spread(i):
        z_copy(i).start()
        y_copy(i).start()
        if i < 2:
            x_copy(i).start()

    lines = rows // 128
    row_acc[...] = jnp.full(row_acc.shape, -1.0, jnp.float32)
    col_acc[...] = jnp.full(col_acc.shape, -1.0, jnp.float32)
    normalise(0)
    normalise(1)
    pl.semaphore_wait(barrier, 6)
    spread(0)
    for i in range(2, CHUNKS):
        normalise(i)
        spread(i - 1)
    owners = (
        (blk(-2), r), (blk(-1 - 2 * odd), r), (blk(-2), far), (b, r),
        (blk(-3 + 2 * odd), r), (blk(-4), r), (blk(-4), far),
    )
    for slot, (block, rep) in enumerate(owners):
        for g in range(lines):
            line = ranks_ref[pl.ds((block * copies + rep) * lines + g, 1), :]
            visit_rank[slot, :, g * 128:(g + 1) * 128] = jnp.broadcast_to(line, (8, 128))
    spread(CHUNKS - 1)
    core_copy().start()
    row_owners = ((b, r), (b, core), (b, far), (b, far_core), (across, r), (across, core))
    for h, (block, rep) in enumerate(row_owners):
        for g in range(lines):
            line = ranks_ref[pl.ds((block * copies + rep) * lines + g, 1), :]
            host_rank[h * rows + g * 128:h * rows + (g + 1) * 128, :] = jnp.broadcast_to(line, (128, 128)).T

    def score(other, slot, start, size, low, span):
        at = pl.ds(pl.multiple_of(start, size), size)
        mine = pl.ds(low, span)
        scores = lax.dot_general(
            host[mine, :], other[at, :], (((1,), (1,)), ((), ())),
            preferred_element_type=jnp.float32,
        )
        line = visit_rank[slot, 0:1, at]
        marks = host_rank[mine, :]
        best = row_acc[mine, :]
        for g in range(size // 128):
            kept = jnp.where(
                line[:, g * 128:(g + 1) * 128] < marks,
                scores[:, g * 128:(g + 1) * 128], jnp.float32(-1.0),
            )
            best = jnp.maximum(best, kept)
            column = jnp.max(kept.reshape(span // 8, 8, 128), axis=0)
            there = pl.ds(pl.multiple_of(start + g * 128, 128), 128)
            col_acc[slot, :, there] = jnp.maximum(col_acc[slot, :, there], column)
        row_acc[mine, :] = best

    wide = 256

    def sweep(other, slot, low, span):
        def step(c, _):
            score(other, slot, c * wide, wide, low, span)
            return 0
        lax.fori_loop(0, rows // wide, step, 0)

    own = host.at[pl.ds(0, rows)]
    beside = host.at[pl.ds(4 * rows, rows)]
    sweep(own, 3, 0, rows)
    core_copy().wait_recv()
    sweep(own, 3, rows, rows)

    for i in range(CHUNKS):
        y_copy(i).wait_recv()
        relay_y(i).start()
        z_copy(i).wait_recv()
        if i < keep:
            side_copy(i).start()
            if i == keep - 1:
                for j in range(2, CHUNKS):
                    x_copy(j).start()
        else:
            up_copy().start()

            @pl.when(odd == 1)
            def _():
                on_v().start()
        if i < 2:
            x_copy(i).wait_recv()
            relay_x(i).start()
        score(visit.at[0], 0, i * part, part, 0, 2 * rows)

    def onward(i):
        side_copy(i).wait_recv()

        @pl.when(even)
        def _():
            on_copy(i).start()

    for i in range(keep - 1):
        onward(i)
    for i in range(CHUNKS):
        relay_y(i).wait_recv()
    sweep(own, 3, 2 * rows, 2 * rows)
    onward(keep - 1)
    up_copy().wait_recv()

    @pl.when(odd == 1)
    def _():
        on_y().start()

    sweep(visit.at[0], 0, 2 * rows, 2 * rows)
    for i in range(keep):
        score(visit.at[1], 1, i * part, part, 2 * rows, 2 * rows)
    half = rows // 2

    def cross(low):
        for h in (4, 5):
            sweep(visit.at[0], 0, h * rows + low, half)
            score(visit.at[2], 2, keep * part, part, h * rows + low, half)

            @pl.when(odd == 1)
            def _():
                score(visit.at[3], 5, keep * part, part, h * rows + low, half)
                score(visit.at[4], 6, keep * part, part, h * rows + low, half)

    for i in range(2):
        relay_x(i).wait_recv()

    @pl.when(odd == 1)
    def _():
        on_v().wait_recv()
        on_y().wait_recv()

    x_copy(2).wait_recv()
    relay_x(2).start()
    cross(0)

    @pl.when(odd == 1)
    def _():
        for i in range(keep):
            score(beside, 4, i * part, part, 0, 4 * rows)

    @pl.when(even)
    def _():
        for i in range(keep - 1):
            on_copy(i).wait_recv()
            score(visit.at[3], 4, i * part, part, 0, 4 * rows)

    x_copy(3).wait_recv()
    relay_x(3).start()

    @pl.when(odd == 1)
    def _():
        score(beside, 4, keep * part, part, 0, 4 * rows)

    @pl.when(even)
    def _():
        on_copy(keep - 1).wait_recv()
        score(visit.at[3], 4, (keep - 1) * part, part, 0, 4 * rows)

    for i in range(2, CHUNKS):
        relay_x(i).wait_recv()

    def col_copy(k):
        return send(col_acc.at[k], col_in.at[k], col_send.at[k], col_recv.at[k], owners[k])

    def row_copy(k):
        return send(row_out.at[k], row_in.at[k], row_send.at[k], row_recv.at[k],
                    row_owners[k + 1])

    def fold(h):
        return jnp.max(row_acc[h * rows:(h + 1) * rows, :].T.reshape(16, 8, rows), axis=0)

    for k in range(3):
        row_out[k] = fold(k + 1)
    col_copy(4).start()
    col_copy(1).start()
    for k in range(3):
        row_copy(k).start()
    cross(half)
    for k in range(3, 5):
        row_out[k] = fold(k + 1)
    col_copy(0).start()
    col_copy(2).start()

    @pl.when(odd == 1)
    def _():
        col_copy(5).start()
        col_copy(6).start()

    for k in range(3, 5):
        row_copy(k).start()
    early = fold(0)
    late = col_acc[3]
    for k in range(5):
        row_copy(k).wait_recv()
        early = jnp.maximum(early, row_in[k])
    for k in (4, 1, 0, 2):
        col_copy(k).wait_recv()
        late = jnp.maximum(late, col_in[k])

    @pl.when(odd == 1)
    def _():
        col_copy(5).wait_recv()
        col_copy(6).wait_recv()
        col_acc[3] = jnp.maximum(col_acc[3], jnp.maximum(col_in[5], col_in[6]))

    late = jnp.maximum(late, col_acc[3])
    early_ref[...] = jnp.max(early, axis=0, keepdims=True)
    late_ref[...] = jnp.max(late, axis=0, keepdims=True)

    core_copy().wait_send()
    for i in range(CHUNKS):
        z_copy(i).wait_send()
        y_copy(i).wait_send()
        x_copy(i).wait_send()
        relay_y(i).wait_send()
        relay_x(i).wait_send()
    for i in range(keep):
        side_copy(i).wait_send()
    up_copy().wait_send()

    @pl.when(even)
    def _():
        for i in range(keep):
            on_copy(i).wait_send()

    @pl.when(odd == 1)
    def _():
        on_v().wait_send()
        on_y().wait_send()
        col_copy(5).wait_send()
        col_copy(6).wait_send()

    for k in range(5):
        row_copy(k).wait_send()
    for k in (4, 1, 0, 2):
        col_copy(k).wait_send()


def shards(embeddings, ranks):
    rows, width = embeddings.shape
    copies = lax.axis_size("rep")
    blocks = lax.axis_size("blk")
    lines = ranks.reshape(-1, 128)
    dma = pltpu.SemaphoreType.DMA
    vmem = pl.BlockSpec(memory_space=pltpu.VMEM)
    early, late = pl.pallas_call(
        functools.partial(kernel, blocks, copies),
        out_shape=[jax.ShapeDtypeStruct((1, rows), jnp.float32)] * 2,
        in_specs=[pl.BlockSpec(memory_space=pltpu.HBM), vmem],
        out_specs=[vmem, vmem],
        scratch_shapes=[
            pltpu.VMEM((rows, width), jnp.float32),
            dma((CHUNKS,)),
            pltpu.VMEM((6 * rows, width), jnp.bfloat16),
            pltpu.VMEM((5, rows, width), jnp.bfloat16),
            pltpu.VMEM((6 * rows, 128), jnp.int32),
            pltpu.VMEM((7, 8, rows), jnp.int32),
            pltpu.VMEM((6 * rows, 128), jnp.float32),
            pltpu.VMEM((7, 8, rows), jnp.float32),
            pltpu.VMEM((7, 8, rows), jnp.float32),
            pltpu.VMEM((5, 8, rows), jnp.float32),
            pltpu.VMEM((5, 8, rows), jnp.float32),
            dma((CHUNKS,)), dma((CHUNKS,)), dma((CHUNKS,)), dma,
            dma((2, CHUNKS)), dma((CHUNKS,)), dma((CHUNKS + 1,)), dma((7,)), dma((5,)),
            dma((5, CHUNKS)), dma((CHUNKS,)), dma((CHUNKS,)), dma, dma((2, CHUNKS)), dma((7,)), dma((5,)),
        ],
        compiler_params=pltpu.CompilerParams(
            collective_id=0, has_side_effects=True, vmem_limit_bytes=63 * 1024 * 1024
        ),
    )(embeddings, lines)
    return early.reshape(rows), late.reshape(rows)


def solution(mesh):
    return jax.shard_map(
        shards,
        mesh=mesh,
        in_specs=(P(("blk", "rep"), None), P()),
        out_specs=(P(("blk", "rep")), P(("blk", "rep"))),
        check_vma=False,
    )
```

time: 51 us -> 53.2 us (1.043)
  Pallas kernels: 47.7 us -> 49.9 us
    pallas_call x1, Pallas kernels: 47.7 us -> 49.9 us  [shards(): pl.pallas_call(functools.partial(kernel, blocks, copies), out_shape=[jax....]
where the time goes in v4:
time: 53.2 us; the launch traced here: 53 us
  Pallas kernels  49.9 us (94%)
  local copies, waits for them, and re-layouts  2.48 us (5%)
  between operations  0.64 us (1%)
    pallas_call x1, Pallas kernels, shards(): pl.pallas_call(functools.partial(kernel, blocks, copies), out_shape=[jax....  49.9 us
    unnamed x2, local copies, waits for them, and re-layouts  2.48 us

profile of v4, /device:TPU:0, one launch (start us, length us, event | category | flops | bytes accessed | tf_op | source)
XLA Modules:
  0.0 53.0 jit_solution(4825819905133906637)
XLA Ops:
  0.6 49.9 %shard_map.41 = (f32[1,512]{1,0:T(1,128)}, f32[1,512]{1,0:T(1,128)}) custom-call(f32[512,768]{1,0:T(8,128)} %emb_ref.1, s32[128,128]{1,0:T(8,128)} %bitcast.3), custom_call_target="tpu_custom_call" | custom-call | tf_op jit(solution)/shard_map/pallas_call | solution.py:358
  50.5 1.2 %copy.6 = f32[512]{0:T(512)} copy(f32[512]{0:T(512)} %bitcast.5) | data formatting | bytes 4096
  51.8 1.2 %copy.7 = f32[512]{0:T(512)} copy(f32[512]{0:T(512)} %bitcast.4) | data formatting | bytes 4096
